TPU v7x, 32 devices: a whole 2x2x4 slice. The times are simulated.
32 devices in a mesh: blk: 8 (over z, y), rep: 4 (over x, core).
Axes of the slice: x: 2, y: 2, z: 4, core: 2. Of those that a mesh axis runs over, the one named last changes fastest.
Arguments:
- tokens: bfloat16 [4096, 8192], P(('blk', 'rep')), may hold values from -6 to 6
- gate_weight: bfloat16 [8, 8192], P('blk'), may hold values from -0.0625 to 0.0625
- up_weight: bfloat16 [8, 8192], P('blk'), may hold values from -0.0625 to 0.0625
- down_weight: bfloat16 [8, 8192], P('blk'), may hold values from -2 to 2
Outputs:
- grad_gate: float32 [8, 8192], P('blk')
- grad_up: float32 [8, 8192], P('blk')
- grad_down: float32 [8, 8192], P('blk')
All inputs are finite; a program needn't handle non-finite values.
Results may differ from a plain program's by a relative error of at most 0.0027.
Values may be sent and summed in bfloat16 or wider, within the bound.
A program may use at most 64 MiB of HBM per device.

v0:
```python
import jax
import jax.numpy as jnp
from jax import lax
from jax.sharding import PartitionSpec as P


def per_device(tokens, gate_weight, up_weight, down_weight):
    tok_rows = tokens.shape[0]
    features = tokens.shape[1]
    cycle_size = lax.axis_size("blk")
    group_size = lax.axis_size("rep")
    loss_scale = float(tok_rows * cycle_size * group_size) ** (-0.5)
    right_numbers = (((1,), (1,)), ((), ()))
    left_numbers = (((0,), (0,)), ((), ()))
    gate_piece = lax.all_gather(gate_weight, "blk", axis=0, tiled=True)
    up_piece = lax.all_gather(up_weight, "blk", axis=0, tiled=True)
    down_piece = lax.all_gather(down_weight, "blk", axis=0, tiled=True)
    gate_pre = lax.dot_general(
        tokens, gate_piece, right_numbers, preferred_element_type=jnp.float32
    )
    up_pre = lax.dot_general(tokens, up_piece, right_numbers, preferred_element_type=jnp.float32)
    hidden_piece = (gate_pre * jax.nn.sigmoid(gate_pre) * up_pre).astype(jnp.bfloat16)
    layer_out = jnp.dot(hidden_piece, down_piece, preferred_element_type=jnp.float32)
    gate_all = gate_pre
    up_all = up_pre
    gate_full = gate_piece
    up_full = up_piece
    down_full = down_piece
    carry = (layer_out, gate_all, up_all, hidden_piece, gate_full, up_full, down_full)
    layer_out, gate_pre, up_pre, hidden, gate_full, up_full, down_full = carry
    cotangent = (layer_out * loss_scale).astype(jnp.bfloat16)
    hidden_grad = lax.dot_general(
        cotangent, down_full, right_numbers, preferred_element_type=jnp.float32
    )
    sigmoid_gate = jax.nn.sigmoid(gate_pre)
    active = gate_pre * sigmoid_gate
    gate_grad = (
        hidden_grad * up_pre * (sigmoid_gate * (1.0 + gate_pre * (1.0 - sigmoid_gate)))
    ).astype(jnp.bfloat16)
    up_grad = (hidden_grad * active).astype(jnp.bfloat16)
    gate_term = lax.dot_general(gate_grad, tokens, left_numbers, preferred_element_type=jnp.float32)
    up_term = lax.dot_general(up_grad, tokens, left_numbers, preferred_element_type=jnp.float32)
    down_term = lax.dot_general(hidden, cotangent, left_numbers, preferred_element_type=jnp.float32)
    shares = lax.psum_scatter(
        jnp.concatenate([gate_term, up_term, down_term], axis=1),
        "blk",
        scatter_dimension=0,
        tiled=True,
    )
    totals = lax.psum(shares, "rep")
    return (totals[:, :features], totals[:, features : 2 * features], totals[:, 2 * features :])


def solution(mesh):
    in_specs = (P(("blk", "rep"), None), P("blk", None), P("blk", None), P("blk", None))
    out_specs = (P("blk", None), P("blk", None), P("blk", None))
    return jax.shard_map(
        per_device, mesh=mesh, in_specs=in_specs, out_specs=out_specs, check_vma=False
    )
```

profile of v0, /device:TPU:0, one launch (start us, length us, event | category | flops | bytes accessed | tf_op | source)
XLA Modules:
  0.0 225.2 jit_solution(10801026277273655064)
XLA Ops:
  7.2 0.0 copy-start
  7.2 0.0 all-reduce.6.cloned.1.call-start
  7.2 32.9 %all-gather.2 = bf16[8,1,8192]{2,1,0:T(2,128)(2,1)S(1)} all-gather(bf16[1,1,8192]{2,1,0:T(2,128)(2,1)} %bitcast.25), channel_id=1, replica_groups=mesh['blk'=8,'rep'=4] {'blk'}, dimensions={0}, use_global_device_ids=true | all-gather | bytes 147456 | tf_op jit(solution)/shard_map/all_gather | solution.py:17
  40.1 30.9 %all-gather = bf16[8,1,8192]{2,1,0:T(2,128)(2,1)S(1)} all-gather(bf16[1,1,8192]{2,1,0:T(2,128)(2,1)} %bitcast.26), channel_id=1, replica_groups=mesh['blk'=8,'rep'=4] {'blk'}, dimensions={0}, use_global_device_ids=true | all-gather | bytes 147456 | tf_op jit(solution)/shard_map/all_gather | solution.py:15
  71.1 30.9 %all-gather.1 = bf16[8,1,8192]{2,1,0:T(2,128)(2,1)S(1)} all-gather(bf16[1,1,8192]{2,1,0:T(2,128)(2,1)} %bitcast.27), channel_id=1, replica_groups=mesh['blk'=8,'rep'=4] {'blk'}, dimensions={0}, use_global_device_ids=true | all-gather | bytes 147456 | tf_op jit(solution)/shard_map/all_gather | solution.py:16
  102.0 0.0 copy-done
  102.0 0.7 fusion.7
  102.7 0.7 multiply_convert_fusion.2
  103.4 0.8 fusion
  104.1 0.6 fusion.1
  104.8 0.4 fusion.20
  105.2 0.4 fusion.14
  105.6 0.0 copy-start.1
  105.6 0.4 fusion.13
  106.0 1.0 pad_maximum_fusion
  106.9 0.0 all-reduce.6.cloned.1.call-update
  107.0 0.0 all-reduce.4.cloned.1.call-start
  107.0 0.0 copy-done.1
  107.0 0.6 dynamic-slice
  107.6 75.8 %all-reduce.6.cloned.1.call-done = f32[8,24576]{1,0:T(8,128)} async-done(((f32[8,24576]{1,0:T(8,128)}), f32[8,24576]{1,0:T(8,128)}) %all-reduce.6.cloned.1.call-update) | async-done | bytes 786448
  183.4 2.5 %constant_dynamic-slice_fusion = f32[1,24576]{1,0:T(1,128)} fusion(f32[8,24576]{1,0:T(8,128)} %all-reduce.6.cloned.1.call-done, u32[]{:T(128)} %bitcast.3), kind=kLoop, calls=%fused_computation.22 | loop fusion | bytes 196612
  185.9 0.0 all-reduce.4.cloned.1.call-update
  185.9 31.0 %all-reduce.4.cloned.1.call-done = f32[1,24576]{1,0:T(1,128)} async-done(((f32[1,24576]{1,0:T(1,128)}), f32[1,24576]{1,0:T(1,128)}) %all-reduce.4.cloned.1.call-update) | async-done | bytes 98320 | tf_op jit(solution)/shard_map/psum | solution.py:50
  216.9 1.4 fusion.19
Async XLA Ops:
  7.2 94.9 %copy-start = (bf16[128,8192]{1,0:T(8,128)(2,1)S(1)}, bf16[128,8192]{1,0:T(8,128)(2,1)}, u32[]{:S(2)}) copy-start(bf16[128,8192]{1,0:T(8,128)(2,1)} %param.4) | copy-start | bytes 6291460
  7.2 176.2 %all-reduce.6.cloned.1.call-start = ((), (), s32[]{:S(2)}) async-start(), calls=%async_computation.1 | async-start | bytes 1572864
  105.6 1.4 copy-start.1
  107.0 109.9 %all-reduce.4.cloned.1.call-start = ((), (), s32[]{:S(2)}) async-start(), calls=%async_computation | async-start | bytes 196608 | tf_op jit(solution)/shard_map/psum | solution.py:50
Sparse Core Ops, SparseCore 0:
  107.1 76.2 all-reduce.5
  186.0 30.8 all-reduce.3
where the time goes:
time: 225 us
  waiting for transfers between devices  107 us (48%)
  blocking collectives  94.8 us (42%)
  between operations  14.1 us (6%)
  local copies, waits for them, and re-layouts  4.51 us (2%)
  matrix products  3.94 us (2%)
    unnamed x3, waiting for transfers between devices  75.8 us
    all_gather x1, blocking collectives, per_device(): down_piece = lax.all_gather(down_weight, 'blk', axis=0, tiled=True)  32.9 us
    psum x1, waiting for transfers between devices, per_device(): totals = lax.psum(shares, 'rep')  31 us
    all_gather x1, blocking collectives, per_device(): gate_piece = lax.all_gather(gate_weight, 'blk', axis=0, tiled=True)  30.9 us
    all_gather x1, blocking collectives, per_device(): up_piece = lax.all_gather(up_weight, 'blk', axis=0, tiled=True)  30.9 us
  transfers between devices with their start and end apart: 2, of which 2 were waited for; matrix products, arithmetic and copies ran while one was open for 0% of the time, Pallas kernels for 0%

commit v1 on v0

--- a/solution.py
+++ b/solution.py
@@ -47,7 +47,7 @@
         scatter_dimension=0,
         tiled=True,
     )
-    totals = lax.psum(shares, "rep")
+    totals = jnp.sum(lax.all_gather(shares, "rep"), axis=0)
     return (totals[:, :features], totals[:, features : 2 * features], totals[:, 2 * features :])
 
 

time: 225 us -> 200 us (0.89)
  waiting for transfers between devices: 107 us -> 75.9 us
  blocking collectives: 94.8 us -> 101 us
    psum x1 -> x0, waiting for transfers between devices: 31 us -> none  [per_device(): totals = lax.psum(shares, 'rep')]
    all_gather x0 -> x1, blocking collectives: none -> 6.44 us  [per_device(): totals = jnp.sum(lax.all_gather(shares, 'rep'), axis=0)]
    unnamed x3 -> x2, waiting for transfers between devices: 75.8 us -> 75.9 us
  transfers between devices with their start and end apart: 2 -> 1, of which waited for: 2 -> 1; matrix products, arithmetic and copies ran while one was open for 0% -> 0% of each run, Pallas kernels for 0% -> 0%
where the time goes in v1:
time: 200 us
  blocking collectives  101 us (50%)
  waiting for transfers between devices  75.9 us (38%)
  between operations  14.1 us (7%)
  matrix products  3.94 us (2%)
  local copies, waits for them, and re-layouts  3.09 us (2%)
    unnamed x2, waiting for transfers between devices  75.9 us
    all_gather x1, blocking collectives, per_device(): down_piece = lax.all_gather(down_weight, 'blk', axis=0, tiled=True)  32.9 us
    all_gather x1, blocking collectives, per_device(): gate_piece = lax.all_gather(gate_weight, 'blk', axis=0, tiled=True)  30.9 us
    all_gather x1, blocking collectives, per_device(): up_piece = lax.all_gather(up_weight, 'blk', axis=0, tiled=True)  30.9 us
    all_gather x1, blocking collectives, per_device(): totals = jnp.sum(lax.all_gather(shares, 'rep'), axis=0)  6.44 us
  transfers between devices with their start and end apart: 1, of which 1 were waited for; matrix products, arithmetic and copies ran while one was open for 0% of the time, Pallas kernels for 0%

profile of v1, /device:TPU:0, one launch (start us, length us, event | category | flops | bytes accessed | tf_op | source)
XLA Modules:
  0.0 199.6 jit_solution(17099611643970499511)
XLA Ops:
  7.2 0.0 copy-start
  7.2 0.0 all-reduce.3.cloned.1.call-start
  7.2 32.9 %all-gather.3 = bf16[8,1,8192]{2,1,0:T(2,128)(2,1)S(1)} all-gather(bf16[1,1,8192]{2,1,0:T(2,128)(2,1)} %bitcast.29), channel_id=1, replica_groups=mesh['blk'=8,'rep'=4] {'blk'}, dimensions={0}, use_global_device_ids=true | all-gather | bytes 147456 | tf_op jit(solution)/shard_map/all_gather | solution.py:17
  40.1 30.9 %all-gather.1 = bf16[8,1,8192]{2,1,0:T(2,128)(2,1)S(1)} all-gather(bf16[1,1,8192]{2,1,0:T(2,128)(2,1)} %bitcast.30), channel_id=1, replica_groups=mesh['blk'=8,'rep'=4] {'blk'}, dimensions={0}, use_global_device_ids=true | all-gather | bytes 147456 | tf_op jit(solution)/shard_map/all_gather | solution.py:15
  71.1 30.9 %all-gather.2 = bf16[8,1,8192]{2,1,0:T(2,128)(2,1)S(1)} all-gather(bf16[1,1,8192]{2,1,0:T(2,128)(2,1)} %bitcast.31), channel_id=1, replica_groups=mesh['blk'=8,'rep'=4] {'blk'}, dimensions={0}, use_global_device_ids=true | all-gather | bytes 147456 | tf_op jit(solution)/shard_map/all_gather | solution.py:16
  102.0 0.0 copy-done
  102.0 0.7 fusion.7
  102.7 0.7 multiply_convert_fusion.2
  103.4 0.8 fusion
  104.1 0.6 fusion.1
  104.8 0.4 fusion.20
  105.2 0.4 fusion.14
  105.6 0.0 copy-start.1
  105.6 0.4 fusion.13
  106.0 1.0 pad_maximum_fusion
  106.9 0.0 all-reduce.3.cloned.1.call-update
  107.0 0.0 copy-done.1
  107.0 0.6 dynamic-slice
  107.6 75.9 %all-reduce.3.cloned.1.call-done = f32[8,24576]{1,0:T(8,128)} async-done(((f32[8,24576]{1,0:T(8,128)}), f32[8,24576]{1,0:T(8,128)}) %all-reduce.3.cloned.1.call-update) | async-done | bytes 786448
  183.4 1.8 dynamic-slice_bitcast_fusion
  185.3 6.4 %all-gather.4 = f32[4,1,24576]{2,1,0:T(1,128)S(1)} all-gather(f32[1,1,24576]{2,1,0:T(1,128)S(1)} %dynamic-slice_bitcast_fusion), channel_id=2, replica_groups=mesh['blk'=8,'rep'=4] {'rep'}, dimensions={0}, use_global_device_ids=true | all-gather | bytes 491520 | tf_op jit(solution)/shard_map/all_gather | solution.py:50
  191.7 0.4 reduce.1
  192.1 0.6 fusion.19
Async XLA Ops:
  7.2 94.9 %copy-start = (bf16[128,8192]{1,0:T(8,128)(2,1)S(1)}, bf16[128,8192]{1,0:T(8,128)(2,1)}, u32[]{:S(2)}) copy-start(bf16[128,8192]{1,0:T(8,128)(2,1)} %param.4) | copy-start | bytes 6291460
  7.2 176.2 %all-reduce.3.cloned.1.call-start = ((), (), s32[]{:S(2)}) async-start(), calls=%async_computation | async-start | bytes 1572864
  105.6 1.4 copy-start.1
Sparse Core Ops, SparseCore 0:
  107.1 76.2 all-reduce.2

commit v2 on v0

--- a/solution.py
+++ b/solution.py
@@ -13,8 +13,13 @@
     right_numbers = (((1,), (1,)), ((), ()))
     left_numbers = (((0,), (0,)), ((), ()))
     gate_piece = lax.all_gather(gate_weight, "blk", axis=0, tiled=True)
-    up_piece = lax.all_gather(up_weight, "blk", axis=0, tiled=True)
-    down_piece = lax.all_gather(down_weight, "blk", axis=0, tiled=True)
+    up_piece, down_piece = jnp.split(
+        lax.all_gather(
+            jnp.concatenate([up_weight, down_weight], axis=1), "blk", axis=0, tiled=True
+        ),
+        [up_weight.shape[1]],
+        axis=1,
+    )
     gate_pre = lax.dot_general(
         tokens, gate_piece, right_numbers, preferred_element_type=jnp.float32
     )

time: 225 us -> 196 us (0.87)
  blocking collectives: 94.8 us -> 64.1 us
    all_gather x2 -> x1, blocking collectives: 63.9 us -> 31.2 us  [per_device(): lax.all_gather(jnp.concatenate([up_weight, down_weight], axis=1), 'blk',...]
where the time goes in v2:
time: 196 us
  waiting for transfers between devices  107 us (55%)
  blocking collectives  64.1 us (33%)
  between operations  14.1 us (7%)
  local copies, waits for them, and re-layouts  4.8 us (2%)
  matrix products  3.92 us (2%)
    unnamed x3, waiting for transfers between devices  75.8 us
    all_gather x1, blocking collectives, per_device(): gate_piece = lax.all_gather(gate_weight, 'blk', axis=0, tiled=True)  32.9 us
    all_gather x1, blocking collectives, per_device(): lax.all_gather(jnp.concatenate([up_weight, down_weight], axis=1), 'blk',...  31.2 us
    psum x1, waiting for transfers between devices, per_device(): totals = lax.psum(shares, 'rep')  31 us
  transfers between devices with their start and end apart: 2, of which 2 were waited for; matrix products, arithmetic and copies ran while one was open for 0% of the time, Pallas kernels for 0%

profile of v2, /device:TPU:0, one launch (start us, length us, event | category | flops | bytes accessed | tf_op | source)
XLA Modules:
  0.0 195.5 jit_solution(5608377386953943517)
XLA Ops:
  7.2 0.0 copy-start
  7.2 0.0 all-reduce.6.cloned.1.call-start
  7.2 32.9 %all-gather = bf16[8,1,8192]{2,1,0:T(2,128)(2,1)S(1)} all-gather(bf16[1,1,8192]{2,1,0:T(2,128)(2,1)} %bitcast.23), channel_id=1, replica_groups=mesh['blk'=8,'rep'=4] {'blk'}, dimensions={0}, use_global_device_ids=true | all-gather | bytes 147456 | tf_op jit(solution)/shard_map/all_gather | solution.py:15
  40.1 0.8 maximum_bitcast_fusion
  41.0 31.2 %all-gather.1 = bf16[8,1,16384]{2,1,0:T(2,128)(2,1)S(1)} all-gather(bf16[1,1,16384]{2,1,0:T(2,128)(2,1)S(1)} %maximum_bitcast_fusion), channel_id=1, replica_groups=mesh['blk'=8,'rep'=4] {'blk'}, dimensions={0}, use_global_device_ids=true | all-gather | bytes 294912 | tf_op jit(solution)/shard_map/all_gather | solution.py:17
  72.2 0.3 copy.14
  72.4 0.0 copy-done
  72.5 0.7 fusion.2
  73.1 0.7 multiply_convert_fusion.2
  73.8 0.8 fusion
  74.6 0.6 fusion.5
  75.2 0.4 fusion.16
  75.6 0.4 fusion.10
  76.0 0.4 fusion.9
  76.4 1.0 pad_maximum_fusion
  77.3 0.0 all-reduce.6.cloned.1.call-update
  77.4 0.0 all-reduce.4.cloned.1.call-start
  77.4 0.0 copy-done.1
  77.4 0.6 dynamic-slice
  78.0 75.8 %all-reduce.6.cloned.1.call-done = f32[8,24576]{1,0:T(8,128)} async-done(((f32[8,24576]{1,0:T(8,128)}), f32[8,24576]{1,0:T(8,128)}) %all-reduce.6.cloned.1.call-update) | async-done | bytes 786448
  153.8 2.5 %constant_dynamic-slice_fusion = f32[1,24576]{1,0:T(1,128)} fusion(f32[8,24576]{1,0:T(8,128)} %all-reduce.6.cloned.1.call-done, u32[]{:T(128)} %bitcast.3), kind=kLoop, calls=%fused_computation.21 | loop fusion | bytes 196612
  156.3 0.0 all-reduce.4.cloned.1.call-update
  156.3 31.0 %all-reduce.4.cloned.1.call-done = f32[1,24576]{1,0:T(1,128)} async-done(((f32[1,24576]{1,0:T(1,128)}), f32[1,24576]{1,0:T(1,128)}) %all-reduce.4.cloned.1.call-update) | async-done | bytes 98320 | tf_op jit(solution)/shard_map/psum | solution.py:55
  187.3 1.4 fusion.15
  (1 shorter events, 0.0 us)
Async XLA Ops:
  7.2 65.3 %copy-start = (bf16[128,8192]{1,0:T(8,128)(2,1)S(1)}, bf16[128,8192]{1,0:T(8,128)(2,1)}, u32[]{:S(2)}) copy-start(bf16[128,8192]{1,0:T(8,128)(2,1)} %param.4) | copy-start | bytes 6291460
  7.2 146.6 %all-reduce.6.cloned.1.call-start = ((), (), s32[]{:S(2)}) async-start(), calls=%async_computation.1 | async-start | bytes 1572864
  76.0 1.4 copy-start.1
  77.4 109.9 %all-reduce.4.cloned.1.call-start = ((), (), s32[]{:S(2)}) async-start(), calls=%async_computation | async-start | bytes 196608 | tf_op jit(solution)/shard_map/psum | solution.py:55
Sparse Core Ops, SparseCore 0:
  77.5 76.2 all-reduce.5
  156.4 30.8 all-reduce.3
